TPU v7x, 32 devices: a whole 2x2x4 slice. The times are simulated.
32 devices in a mesh: orig: 8 (over z, y), link: 4 (over x, core).
Axes of the slice: x: 2, y: 2, z: 4, core: 2. Of those that a mesh axis runs over, the one named last changes fastest.
Arguments:
- background: bfloat16 [16384, 256], P('orig'), may hold values from -6 to 6
- live_counts: int32 [128], P('orig'), may hold values from 1 to 128
- patterns: bfloat16 [4, 256, 128, 128], P('link', 'orig'), may hold values from -0.0390625 to 0.0390625
- pattern_ids: int32 [4, 128, 12], P('link', 'orig'), may hold values from 0 to 31
- link_targets: int32 [4, 128, 12], P('link', 'orig'), may hold values from 0 to 7
- counts_obs: float32 [4, 1024], P('link', 'orig'), may hold values from -6 to 6
- obs_var: float32 [4, 1024], P('link', 'orig'), may hold values from 1 to 10
Outputs:
- analysis: bfloat16 [16384, 256], P(('orig', 'link'))
All inputs are finite; a program needn't handle non-finite values. Where the computation divides by a largest or mean magnitude, that divisor is 1e-20 or more.
Results may differ from a plain program's by a relative error of at most 0.001.
Values sent between devices are 32-bit elements; how exact they have to be, the bound alone decides.
A program may use at most 64 MiB of HBM per device.

v0:
```python
import functools

import jax
import jax.numpy as jnp
from jax import lax
from jax.experimental import pallas as pl
from jax.experimental.pallas import tpu as pltpu
from jax.sharding import PartitionSpec as P

NS_ITERS = 4
CUTS = 4
WIDE_GRANT = 67043328 - 900 * 1024
MESH = pl.DeviceIdType.MESH
F32 = jnp.float32
BF16 = jnp.bfloat16


def repeat(count, body):
    if count <= 16:
        for step in range(count):
            body(step)
    else:
        lax.fori_loop(0, count, lambda step, carry: (body(step), carry)[1], 0)


def xor(a, b, size):
    total = 0
    bit = 1
    while bit < size:
        total = total + ((a // bit) % 2 + (b // bit) % 2) % 2 * bit
        bit *= 2
    return total


def split(x):
    high = x.astype(BF16)
    return high, (x - high.astype(F32)).astype(BF16)


def mm3(a, b):
    a_high, a_low = split(a)
    b_high, b_low = split(b)
    return (
        jnp.dot(a_high, b_low, preferred_element_type=F32)
        + jnp.dot(a_low, b_high, preferred_element_type=F32)
    ) + jnp.dot(a_high, b_high, preferred_element_type=F32)


def predict_kernel(
    ids_ref, targets_ref, counts_ref, tiles_hbm, states_hbm, out_ref, tiles_ref, states_ref, tiles_sem, states_sem
):
    slots = ids_ref.shape[0]
    blocks, rows, members = states_ref.shape
    group = blocks // states_sem.shape[0]
    tiles_copy = pltpu.make_async_copy(tiles_hbm, tiles_ref, tiles_sem)
    tiles_copy.start()

    def states_copy(part):
        where = pl.ds(part * group, group)
        return pltpu.make_async_copy(states_hbm.at[where], states_ref.at[where], states_sem.at[part])

    for part in range(blocks // group):
        states_copy(part).start()
    out_ref[...] = jnp.zeros_like(out_ref)
    position = lax.broadcasted_iota(jnp.int32, (rows, members), 0)
    tiles_copy.wait()

    def add_block(block, carry):
        states = states_ref[block]
        states = jnp.where(position < counts_ref[block], states, jnp.zeros_like(states))
        for slot in range(slots):
            target = targets_ref[slot, 0, block]
            term = jnp.dot(tiles_ref[ids_ref[slot, 0, block]], states, preferred_element_type=F32)
            out_ref[target] = out_ref[target] + term
        return carry

    def add_part(part, carry):
        states_copy(part).wait()
        return lax.fori_loop(
            0, group, lambda step, kept: add_block(part * group + step, kept), carry, unroll=2
        )

    lax.fori_loop(0, blocks // group, add_part, 0)


def transform_of(gram, forcing):
    members = gram.shape[0]
    row = lax.broadcasted_iota(jnp.int32, (members, members), 0)
    column = lax.broadcasted_iota(jnp.int32, (members, members), 1)
    identity = (row == column).astype(F32)
    system = identity + gram * (1.0 / (members - 1.0))
    bound = jnp.max(jnp.sum(jnp.abs(system), axis=1, keepdims=True), axis=0, keepdims=True)
    root = system / bound
    middle = 1.5 * identity - 0.5 * root
    inverse = middle
    root = mm3(root, middle)
    for sweep in range(1, NS_ITERS):
        middle = 1.5 * identity - 0.5 * mm3(inverse, root)
        if sweep < NS_ITERS - 1:
            root = mm3(root, middle)
        inverse = mm3(middle, inverse)
    inner = mm3(jnp.broadcast_to(forcing, (8, members)), inverse)
    mean_weights = mm3(inner, inverse)[0:1] / (bound * (members - 1.0))
    whole = inverse / jnp.sqrt(bound) + jnp.broadcast_to(mean_weights, (members, members)).T
    return whole + (1.0 - jnp.sum(whole, axis=0, keepdims=True)) / members


def gram_kernel(
    n_orig, n_link, term_hbm, obs_ref, var_ref, out_ref,
    term_ref, term_sem, first_in, sums, side_in, far_in, gram_ref, half_in, half_ref, piece_in, piece_ref, final_ref,
    send1, recv1, send2, recv2, send7, recv7, send3, recv3, send4, recv4, send5, recv5, send6, recv6,
):
    orig = lax.axis_index("orig")
    link = lax.axis_index("link")
    rows = obs_ref.shape[1]
    members = term_ref.shape[1]
    half = members // 2
    pairs = n_orig // 2
    parity = orig % 2
    place = orig // 2
    across = orig + 1 - 2 * parity
    side = link % 2
    twin = link + 1 - 2 * side
    ring = n_orig * n_link // 2
    rank = (link // 2) * n_orig + orig
    owners = min(ring, half // 8)
    piece = half // owners

    def device_of(other):
        return (other % n_orig, (other // n_orig) * 2 + side)

    load = pltpu.make_async_copy(term_hbm, term_ref, term_sem)
    load.start()
    near = place % 2
    far = place // 2
    n_far = pairs // 2
    barrier = pltpu.get_barrier_semaphore()

    def greet(other_orig, other_link):
        pl.semaphore_signal(barrier, inc=1, device_id=(other_orig, other_link), device_id_type=MESH)

    greet(across, link)
    greet(2 * (far * 2 + 1 - near) + parity, link)
    repeat(n_far - 1, lambda step: greet(2 * (xor(far, step + 1, n_far) * 2 + near) + parity, link))
    repeat(n_link - 1, lambda step: greet(orig, (link + step + 1) % n_link))
    pl.semaphore_wait(barrier, n_far + n_link)
    load.wait()

    cuts = max(1, min(CUTS, rows // 8))
    cut_rows = rows // cuts
    steps = n_far * cuts

    def owner(step, flip):
        other = xor(far, n_far - 1 - step // cuts, n_far)
        return other * 2 + (near + flip) % 2

    def term_rows(index, step):
        return pl.ds(pl.multiple_of(index * rows + step % cuts * cut_rows, cut_rows), cut_rows)

    def cut(step):
        return pl.ds(pl.multiple_of(step % cuts * cut_rows, cut_rows), cut_rows)

    def slot(step, flip):
        return step // cuts * 2 + 1 - flip

    def first(step, flip):
        index = slot(step, flip) * cuts + step % cuts
        return pltpu.make_async_remote_copy(
            src_ref=term_ref.at[term_rows(2 * owner(step, flip) + 1 - parity, step)],
            dst_ref=first_in.at[slot(step, flip), cut(step)],
            send_sem=send1.at[index], recv_sem=recv1.at[index],
            device_id=(across, link), device_id_type=MESH,
        )

    def beside(step):
        return pltpu.make_async_remote_copy(
            src_ref=sums.at[slot(step, 1), cut(step)], dst_ref=side_in.at[step // cuts, cut(step)],
            send_sem=send2.at[step], recv_sem=recv2.at[step],
            device_id=(2 * (far * 2 + 1 - near) + parity, link), device_id_type=MESH,
        )

    def beyond(step):
        return pltpu.make_async_remote_copy(
            src_ref=sums.at[slot(step, 0), cut(step)], dst_ref=far_in.at[step // cuts, cut(step)],
            send_sem=send7.at[step], recv_sem=recv7.at[step],
            device_id=(2 * owner(step, 0) + parity, link), device_id_type=MESH,
        )

    remote = steps - cuts
    lag = min(2, remote, cuts)

    def first_start(step):
        first(step, 1).start()
        first(step, 0).start()

    repeat(remote, first_start)
    repeat(cuts, lambda step: first(step + remote, 1).start())
    repeat(cuts, lambda step: first(step + remote, 0).start())

    def add_first(step, flip):
        first(step, flip).wait_recv()
        sums[slot(step, flip), cut(step)] = (
            term_ref[term_rows(2 * owner(step, flip) + parity, step)] + first_in[slot(step, flip), cut(step)]
        )
        if flip:
            beside(step).start()

    def add_beside(step):
        beside(step).wait_recv()
        sums[slot(step, 0), cut(step)] = sums[slot(step, 0), cut(step)] + side_in[step // cuts, cut(step)]

    def pass_on(step):
        add_beside(step)
        beyond(step).start()

    def enter(step):
        add_first(step, 1)
        add_first(step, 0)

    repeat(lag, enter)

    def middle_step(step):
        enter(step + lag)
        pass_on(step)

    repeat(remote - lag, middle_step)
    for step in range(cuts):
        add_first(step + remote, 1)
        if step < lag:
            pass_on(step + (remote - lag))
    for step in range(cuts):
        add_first(step + remote, 0)
        add_beside(step + remote)

    def gather(step):
        beyond(step).wait_recv()
        sums[pairs - 1, cut(step)] = sums[pairs - 1, cut(step)] + far_in[step // cuts, cut(step)]

    repeat(remote, gather)

    predicted = sums[pairs - 1]
    turned = predicted.T
    weights = 1.0 / var_ref[...]
    mean_row = jnp.sum(turned, axis=0, keepdims=True) / members
    spread = predicted - jnp.sum(predicted, axis=1, keepdims=True) / members
    spread_t = turned - mean_row
    gram_ref[...] = mm3(spread_t * weights, spread)
    pull = jnp.broadcast_to(weights * (obs_ref[...] - mean_row), (8, rows))
    forcing = mm3(pull, spread)
    gram_ref[pl.ds(half, 1), 0:half] = forcing[0:1, 0:half]
    gram_ref[pl.ds(half + 1, 1), 0:half] = forcing[0:1, half:]

    swap = pltpu.make_async_remote_copy(
        src_ref=gram_ref.at[pl.ds(pl.multiple_of((1 - side) * half, half), half)], dst_ref=half_in,
        send_sem=send3, recv_sem=recv3, device_id=(orig, twin), device_id_type=MESH,
    )
    swap.start()
    swap.wait_recv()
    half_ref[...] = gram_ref[pl.ds(pl.multiple_of(side * half, half), half)] + half_in[...]

    def scatter(step):
        other = xor(rank, ring - 1 - step, ring)
        return pltpu.make_async_remote_copy(
            src_ref=half_ref.at[pl.ds(pl.multiple_of(other * piece, piece), piece)], dst_ref=piece_in.at[step],
            send_sem=send4.at[step], recv_sem=recv4.at[step],
            device_id=device_of(other), device_id_type=MESH,
        )

    def spread_out(source, step, other):
        where = pl.ds(pl.multiple_of(side * half + source * piece, piece), piece)
        return pltpu.make_async_remote_copy(
            src_ref=piece_ref, dst_ref=final_ref.at[where],
            send_sem=send5.at[step], recv_sem=recv5.at[step],
            device_id=device_of(other), device_id_type=MESH,
        )

    def guarded(condition, action):
        if owners == ring:
            action()
        else:
            pl.when(condition)(action)

    def scatter_start(step):
        guarded(xor(rank, ring - 1 - step, ring) < owners, lambda: scatter(step).start())

    repeat(ring - 1, scatter_start)

    def reduce_piece():
        piece_ref[...] = half_ref[pl.ds(pl.multiple_of(rank * piece, piece), piece)]

        def add(step):
            scatter(step).wait_recv()
            piece_ref[...] = piece_ref[...] + piece_in[step]

        repeat(ring - 1, add)
        repeat(ring - 1, lambda step: spread_out(rank, step, xor(rank, ring - 1 - step, ring)).start())
        final_ref[pl.ds(pl.multiple_of(side * half + rank * piece, piece), piece)] = piece_ref[...]

    guarded(rank < owners, reduce_piece)

    def spread_wait(step):
        other = xor(rank, ring - 1 - step, ring)
        guarded(other < owners, lambda: spread_out(other, step, other).wait_recv())

    repeat(ring - 1, spread_wait)
    mine = pl.ds(pl.multiple_of(side * half, half), half)
    share = pltpu.make_async_remote_copy(
        src_ref=final_ref.at[mine], dst_ref=final_ref.at[mine],
        send_sem=send6, recv_sem=recv6, device_id=(orig, twin), device_id_type=MESH,
    )
    share.start()
    share.wait_recv()

    out_ref[...] = final_ref[...]

    def first_end(step):
        first(step, 1).wait_send()
        first(step, 0).wait_send()
        beside(step).wait_send()

    repeat(steps, first_end)
    repeat(remote, lambda step: beyond(step).wait_send())
    swap.wait_send()

    def scatter_end(step):
        guarded(xor(rank, ring - 1 - step, ring) < owners, lambda: scatter(step).wait_send())

    repeat(ring - 1, scatter_end)
    guarded(
        rank < owners,
        lambda: repeat(
            ring - 1, lambda step: spread_out(rank, step, xor(rank, ring - 1 - step, ring)).wait_send()
        ),
    )
    share.wait_send()


def update_kernel(counts_ref, final_ref, states_hbm, out_ref, states_ref, states_sem):
    link = lax.axis_index("link")
    own_rows, members = out_ref.shape
    half = members // 2
    fetch = pltpu.make_async_copy(
        states_hbm.at[pl.ds(pl.multiple_of(link * own_rows, own_rows), own_rows)], states_ref, states_sem
    )
    fetch.start()
    upper = final_ref[0:half, half:]
    gram = jnp.concatenate(
        [final_ref[0:half, :], jnp.concatenate([upper.T, final_ref[half:, half:]], axis=1)], axis=0
    )
    forcing = jnp.concatenate(
        [final_ref[pl.ds(half, 1), 0:half], final_ref[pl.ds(half + 1, 1), 0:half]], axis=1
    )
    high, low = split(transform_of(gram, forcing))
    fetch.wait()
    block_rows = states_hbm.shape[0] // counts_ref.shape[0]
    blocks = own_rows // block_rows
    position = lax.broadcasted_iota(jnp.int32, (block_rows, members), 0)
    for index in range(blocks):
        states = states_ref[index * block_rows : (index + 1) * block_rows]
        updated = jnp.dot(states, low, preferred_element_type=F32) + jnp.dot(
            states, high, preferred_element_type=F32
        )
        living = position < counts_ref[link * blocks + index]
        out_ref[index * block_rows : (index + 1) * block_rows] = jnp.where(
            living, updated, states.astype(F32)
        ).astype(BF16)


def per_device(background, live_counts, patterns, pattern_ids, link_targets, counts_obs, obs_var):
    n_orig = lax.axis_size("orig")
    n_link = lax.axis_size("link")
    states_dev, members = background.shape
    blocks_dev = live_counts.shape[0]
    block_rows = states_dev // blocks_dev
    link_rows = patterns.shape[2]
    rows = counts_obs.shape[1]
    link_blocks = rows * n_orig // link_rows
    vmem = pl.BlockSpec(memory_space=pltpu.VMEM)
    smem = pl.BlockSpec(memory_space=pltpu.SMEM)
    hbm = pl.BlockSpec(memory_space=pl.ANY)
    dma = pltpu.SemaphoreType.DMA
    grant = pltpu.CompilerParams(vmem_limit_bytes=WIDE_GRANT)
    term = pl.pallas_call(
        predict_kernel,
        out_shape=jax.ShapeDtypeStruct((link_blocks, link_rows, members), F32),
        in_specs=[smem, smem, smem, hbm, hbm],
        out_specs=vmem,
        scratch_shapes=[
            pltpu.VMEM(patterns.shape[1:], BF16),
            pltpu.VMEM((blocks_dev, block_rows, members), BF16),
            dma,
            dma((4,)),
        ],
    )(
        jnp.transpose(pattern_ids, (2, 0, 1)), jnp.transpose(link_targets, (2, 0, 1)), live_counts,
        patterns[0], background.reshape(blocks_dev, block_rows, members),
    )
    pairs = n_orig // 2
    ring = n_orig * n_link // 2
    half = members // 2
    piece = half // min(ring, half // 8)
    cuts = max(1, min(CUTS, rows // 8))
    steps = pairs // 2 * cuts
    gram = pl.pallas_call(
        functools.partial(gram_kernel, n_orig, n_link),
        out_shape=jax.ShapeDtypeStruct((members, members), F32),
        in_specs=[hbm, vmem, vmem],
        out_specs=vmem,
        scratch_shapes=[
            pltpu.VMEM((link_blocks * link_rows, members), F32),
            dma,
            pltpu.VMEM((pairs, rows, members), F32),
            pltpu.VMEM((pairs, rows, members), F32),
            pltpu.VMEM((pairs // 2, rows, members), F32),
            pltpu.VMEM((pairs // 2, rows, members), F32),
            pltpu.VMEM((members, members), F32),
            pltpu.VMEM((half, members), F32),
            pltpu.VMEM((half, members), F32),
            pltpu.VMEM((ring - 1, piece, members), F32),
            pltpu.VMEM((piece, members), F32),
            pltpu.VMEM((members, members), F32),
            dma((2 * steps,)), dma((2 * steps,)),
            dma((steps,)), dma((steps,)),
            dma((steps,)), dma((steps,)),
            dma, dma,
            dma((ring,)), dma((ring,)),
            dma((ring,)), dma((ring,)),
            dma, dma,
        ],
        compiler_params=pltpu.CompilerParams(
            collective_id=0, has_side_effects=True, vmem_limit_bytes=WIDE_GRANT
        ),
    )(term.reshape(link_blocks * link_rows, members), counts_obs, obs_var)
    own_rows = states_dev // n_link
    return pl.pallas_call(
        update_kernel,
        out_shape=jax.ShapeDtypeStruct((own_rows, members), BF16),
        in_specs=[smem, vmem, hbm],
        out_specs=vmem,
        scratch_shapes=[pltpu.VMEM((own_rows, members), BF16), dma],
        compiler_params=grant,
    )(live_counts, gram, background)


def solution(mesh):
    placed = (
        P("orig", None),
        P("orig"),
        P("link", "orig", None, None),
        P("link", "orig", None),
        P("link", "orig", None),
        P("link", "orig"),
        P("link", "orig"),
    )
    return jax.shard_map(
        per_device, mesh=mesh, in_specs=placed, out_specs=P(("orig", "link"), None), check_vma=False
    )
```

profile of v0, /device:TPU:0, one launch (start us, length us, event | category | flops | bytes accessed | tf_op | source)
XLA Modules:
  0.0 48.1 jit_solution(6671381586942723668)
XLA Ops:
  0.0 8.0 %shard_map.73 = f32[8,128,256]{2,1,0:T(8,128)} custom-call(s32[12,1,16]{2,1,0:T(1,128)} %bitcast.8, s32[12,1,16]{2,1,0:T(1,128)} %bitcast.9, s32[16]{0:T(128)} %counts_ref.3, bf16[32,128,128]{2,1,0:T(8,128)(2,1)} %bitcast.7, bf16[16,128,256]{2,1,0:T(8,128)(2,1)} %bitcast.5), custom_call_target="tpu_custom_call" | custom-call | tf_op jit(solution)/shard_map/pallas_call | solution.py:383
  8.0 35.1 %shard_map.74.final_ref = f32[256,256]{1,0:T(8,128)} custom-call(f32[1024,256]{1,0:T(8,128)} %bitcast.6, f32[1,128]{1,0:T(1,128)} %obs_ref.1, f32[1,128]{1,0:T(1,128)} %var_ref.1), custom_call_target="tpu_custom_call" | custom-call | tf_op jit(solution)/shard_map/pallas_call | solution.py:404
  43.2 5.0 %shard_map.75 = bf16[512,256]{1,0:T(8,128)(2,1)} custom-call(s32[16]{0:T(128)} %counts_ref.3, f32[256,256]{1,0:T(8,128)} %shard_map.74.final_ref, bf16[2048,256]{1,0:T(8,128)(2,1)} %states_hbm.1), custom_call_target="tpu_custom_call" | custom-call | tf_op jit(solution)/shard_map/pallas_call | solution.py:435
where the time goes:
time: 48.4 us; the launch traced here: 48.1 us
  Pallas kernels  48.1 us (99%)
    pallas_call x1, Pallas kernels, per_device(): pl.pallas_call(functools.partial(gram_kernel, n_orig, n_link), out_shape=...  35.1 us
    pallas_call x1, Pallas kernels, per_device(): pl.pallas_call(predict_kernel, out_shape=jax.ShapeDtypeStruct((link_block...  8.03 us
    pallas_call x1, Pallas kernels, per_device(): pl.pallas_call(update_kernel, out_shape=jax.ShapeDtypeStruct((own_rows, m...  4.97 us

commit v1 on v0

--- a/solution.py
+++ b/solution.py
@@ -9,6 +9,7 @@
 
 NS_ITERS = 4
 CUTS = 4
+UNROLL = 2
 WIDE_GRANT = 67043328 - 900 * 1024
 MESH = pl.DeviceIdType.MESH
 F32 = jnp.float32
@@ -46,41 +47,82 @@
     ) + jnp.dot(a_high, b_high, preferred_element_type=F32)
 
 
-def predict_kernel(
-    ids_ref, targets_ref, counts_ref, tiles_hbm, states_hbm, out_ref, tiles_ref, states_ref, tiles_sem, states_sem
-):
+def sort_slots(ids_ref, targets_ref, words_ref, bits):
     slots = ids_ref.shape[0]
-    blocks, rows, members = states_ref.shape
-    group = blocks // states_sem.shape[0]
-    tiles_copy = pltpu.make_async_copy(tiles_hbm, tiles_ref, tiles_sem)
-    tiles_copy.start()
-
-    def states_copy(part):
-        where = pl.ds(part * group, group)
-        return pltpu.make_async_copy(states_hbm.at[where], states_ref.at[where], states_sem.at[part])
-
-    for part in range(blocks // group):
-        states_copy(part).start()
-    out_ref[...] = jnp.zeros_like(out_ref)
-    position = lax.broadcasted_iota(jnp.int32, (rows, members), 0)
-    tiles_copy.wait()
-
-    def add_block(block, carry):
-        states = states_ref[block]
-        states = jnp.where(position < counts_ref[block], states, jnp.zeros_like(states))
+    blocks = ids_ref.shape[2]
+    per_word = 31 // bits
+    n_words = pl.cdiv(slots, per_word)
+
+    def sort_block(block, carry):
+        amounts = [targets_ref[slot, 0, block] * 4 for slot in range(slots)]
+        ones = [jnp.left_shift(1, amount) for amount in amounts]
+        tally = functools.reduce(lambda a, b: a + b, ones)
+        starts = jnp.int32(0)
+        for shift in range(1, 8):
+            starts = starts + jnp.left_shift(tally, 4 * shift)
+        place = starts
+        words = [jnp.int32(0) for _ in range(n_words)]
         for slot in range(slots):
-            target = targets_ref[slot, 0, block]
-            term = jnp.dot(tiles_ref[ids_ref[slot, 0, block]], states, preferred_element_type=F32)
-            out_ref[target] = out_ref[target] + term
+            rank = jnp.bitwise_and(jnp.right_shift(place, amounts[slot]), 15)
+            place = place + ones[slot]
+            tile = ids_ref[slot, 0, block]
+            for word in range(n_words):
+                local = rank - word * per_word
+                inside = (local >= 0) & (local < per_word)
+                shift = jnp.where(inside, local * bits, 0)
+                words[word] = words[word] + jnp.where(inside, jnp.left_shift(tile, shift), 0)
+        words_ref[0, block] = starts
+        words_ref[1, block] = place
+        for word in range(n_words):
+            words_ref[2 + word, block] = words[word]
         return carry
 
-    def add_part(part, carry):
-        states_copy(part).wait()
-        return lax.fori_loop(
-            0, group, lambda step, kept: add_block(part * group + step, kept), carry, unroll=2
-        )
-
-    lax.fori_loop(0, blocks // group, add_part, 0)
+    lax.fori_loop(0, blocks, sort_block, 0)
+
+
+def predict_cut(words_ref, tiles_ref, states_ref, prefix_refs, term_ref, cut_index, cut_rows, slots, bits):
+    link_rows, block_rows = tiles_ref.shape[1:]
+    link_blocks = term_ref.shape[0] // link_rows
+    per_word = 31 // bits
+    span = len(prefix_refs)
+    steps = states_ref.shape[0] // (span * block_rows)
+    rows_at = pl.ds(cut_index * cut_rows, cut_rows)
+
+    def add_step(step, carry):
+        highs, lows = [], []
+        for index, prefix_ref in enumerate(prefix_refs):
+            block = step * span + index
+            words = [words_ref[2 + word, block] for word in range(pl.cdiv(slots, per_word))]
+            total = jnp.zeros((cut_rows, block_rows), F32)
+            for slot in range(slots):
+                shifted = jnp.right_shift(words[slot // per_word], slot % per_word * bits)
+                tile = jnp.bitwise_and(shifted, 2**bits - 1)
+                total = total + tiles_ref[tile, rows_at, :].astype(F32)
+                prefix_ref[slot + 1, 0:cut_rows] = total
+            starts, ends = words_ref[0, block], words_ref[1, block]
+            high_parts, low_parts = [], []
+            for target in range(link_blocks):
+                first = jnp.bitwise_and(jnp.right_shift(starts, 4 * target), 15)
+                last = jnp.bitwise_and(jnp.right_shift(ends, 4 * target), 15)
+                high, low = split(prefix_ref[last, 0:cut_rows] - prefix_ref[first, 0:cut_rows])
+                high_parts.append(high)
+                low_parts.append(low)
+            highs.append(jnp.concatenate(high_parts, axis=0))
+            lows.append(jnp.concatenate(low_parts, axis=0))
+        states = states_ref[pl.ds(pl.multiple_of(step * span * block_rows, span * block_rows), span * block_rows)]
+        product = jnp.dot(jnp.concatenate(highs, axis=1), states, preferred_element_type=F32) + jnp.dot(
+            jnp.concatenate(lows, axis=1), states, preferred_element_type=F32
+        )
+        for target in range(link_blocks):
+            where = pl.ds(target * link_rows + cut_index * cut_rows, cut_rows)
+            term_ref[where] = term_ref[where] + product[target * cut_rows : (target + 1) * cut_rows]
+        return carry
+
+    for target in range(link_blocks):
+        term_ref[pl.ds(target * link_rows + cut_index * cut_rows, cut_rows)] = jnp.zeros(
+            (cut_rows, term_ref.shape[1]), F32
+        )
+    lax.fori_loop(0, steps, add_step, 0, unroll=UNROLL)
 
 
 def transform_of(gram, forcing):
@@ -106,8 +148,8 @@
 
 
 def gram_kernel(
-    n_orig, n_link, term_hbm, obs_ref, var_ref, out_ref,
-    term_ref, term_sem, first_in, sums, side_in, far_in, gram_ref, half_in, half_ref, piece_in, piece_ref, final_ref,
+    n_orig, n_link, cuts, ids_ref, targets_ref, counts_ref, tiles_hbm, states_hbm, obs_ref, var_ref, out_ref,
+    tiles_ref, states_ref, tiles_sem, states_sem, even_ref, odd_ref, words_ref, term_ref, first_in, sums, side_in, far_in, gram_ref, half_in, half_ref, piece_in, piece_ref, final_ref,
     send1, recv1, send2, recv2, send7, recv7, send3, recv3, send4, recv4, send5, recv5, send6, recv6,
 ):
     orig = lax.axis_index("orig")
@@ -129,8 +171,10 @@
     def device_of(other):
         return (other % n_orig, (other // n_orig) * 2 + side)
 
-    load = pltpu.make_async_copy(term_hbm, term_ref, term_sem)
-    load.start()
+    load_states = pltpu.make_async_copy(states_hbm, states_ref, states_sem)
+    load_states.start()
+    load_tiles = pltpu.make_async_copy(tiles_hbm, tiles_ref, tiles_sem)
+    load_tiles.start()
     near = place % 2
     far = place // 2
     n_far = pairs // 2
@@ -143,10 +187,26 @@
     greet(2 * (far * 2 + 1 - near) + parity, link)
     repeat(n_far - 1, lambda step: greet(2 * (xor(far, step + 1, n_far) * 2 + near) + parity, link))
     repeat(n_link - 1, lambda step: greet(orig, (link + step + 1) % n_link))
-    pl.semaphore_wait(barrier, n_far + n_link)
-    load.wait()
-
-    cuts = max(1, min(CUTS, rows // 8))
+
+    slots = ids_ref.shape[0]
+    blocks = counts_ref.shape[0]
+    block_rows = states_ref.shape[0] // blocks
+    bits = max(1, (tiles_ref.shape[0] - 1).bit_length())
+    sort_slots(ids_ref, targets_ref, words_ref, bits)
+    for prefix_ref in (even_ref, odd_ref):
+        prefix_ref[...] = jnp.zeros(prefix_ref.shape, F32)
+    position = lax.broadcasted_iota(jnp.int32, (block_rows, members), 0)
+    load_states.wait()
+
+    def mask_block(block, carry):
+        where = pl.ds(pl.multiple_of(block * block_rows, block_rows), block_rows)
+        states = states_ref[where]
+        states_ref[where] = jnp.where(position < counts_ref[block], states, jnp.zeros_like(states))
+        return carry
+
+    lax.fori_loop(0, blocks, mask_block, 0, unroll=2)
+    load_tiles.wait()
+
     cut_rows = rows // cuts
     steps = n_far * cuts
 
@@ -189,11 +249,19 @@
     remote = steps - cuts
     lag = min(2, remote, cuts)
 
-    def first_start(step):
-        first(step, 1).start()
-        first(step, 0).start()
-
-    repeat(remote, first_start)
+    for index in range(cuts):
+        predict_cut(
+            words_ref, tiles_ref, states_ref, (even_ref, odd_ref), term_ref,
+            index, tiles_ref.shape[1] // cuts, slots, bits,
+        )
+        if index == 0:
+            pl.semaphore_wait(barrier, n_far + n_link)
+
+        def first_start(step):
+            first(step * cuts + index, 1).start()
+            first(step * cuts + index, 0).start()
+
+        repeat(n_far - 1, first_start)
     repeat(cuts, lambda step: first(step + remote, 1).start())
     repeat(cuts, lambda step: first(step + remote, 0).start())
 
@@ -380,35 +448,27 @@
     hbm = pl.BlockSpec(memory_space=pl.ANY)
     dma = pltpu.SemaphoreType.DMA
     grant = pltpu.CompilerParams(vmem_limit_bytes=WIDE_GRANT)
-    term = pl.pallas_call(
-        predict_kernel,
-        out_shape=jax.ShapeDtypeStruct((link_blocks, link_rows, members), F32),
-        in_specs=[smem, smem, smem, hbm, hbm],
-        out_specs=vmem,
-        scratch_shapes=[
-            pltpu.VMEM(patterns.shape[1:], BF16),
-            pltpu.VMEM((blocks_dev, block_rows, members), BF16),
-            dma,
-            dma((4,)),
-        ],
-    )(
-        jnp.transpose(pattern_ids, (2, 0, 1)), jnp.transpose(link_targets, (2, 0, 1)), live_counts,
-        patterns[0], background.reshape(blocks_dev, block_rows, members),
-    )
     pairs = n_orig // 2
     ring = n_orig * n_link // 2
     half = members // 2
     piece = half // min(ring, half // 8)
-    cuts = max(1, min(CUTS, rows // 8))
+    cuts = CUTS if rows == link_rows else 1
+    slots = pattern_ids.shape[2]
     steps = pairs // 2 * cuts
     gram = pl.pallas_call(
-        functools.partial(gram_kernel, n_orig, n_link),
+        functools.partial(gram_kernel, n_orig, n_link, cuts),
         out_shape=jax.ShapeDtypeStruct((members, members), F32),
-        in_specs=[hbm, vmem, vmem],
+        in_specs=[smem, smem, smem, hbm, hbm, vmem, vmem],
         out_specs=vmem,
         scratch_shapes=[
+            pltpu.VMEM(patterns.shape[1:], BF16),
+            pltpu.VMEM((states_dev, members), BF16),
+            dma,
+            dma,
+            pltpu.VMEM((16, link_rows // cuts, block_rows), F32),
+            pltpu.VMEM((16, link_rows // cuts, block_rows), F32),
+            pltpu.SMEM((8, blocks_dev), jnp.int32),
             pltpu.VMEM((link_blocks * link_rows, members), F32),
-            dma,
             pltpu.VMEM((pairs, rows, members), F32),
             pltpu.VMEM((pairs, rows, members), F32),
             pltpu.VMEM((pairs // 2, rows, members), F32),
@@ -430,7 +490,10 @@
         compiler_params=pltpu.CompilerParams(
             collective_id=0, has_side_effects=True, vmem_limit_bytes=WIDE_GRANT
         ),
-    )(term.reshape(link_blocks * link_rows, members), counts_obs, obs_var)
+    )(
+        jnp.transpose(pattern_ids, (2, 0, 1)), jnp.transpose(link_targets, (2, 0, 1)), live_counts,
+        patterns[0], background, counts_obs, obs_var,
+    )
     own_rows = states_dev // n_link
     return pl.pallas_call(
         update_kernel,

time: 48.4 us -> 42.4 us (0.88)
  Pallas kernels: 48.1 us -> 42.3 us
    pallas_call x2 -> x1, Pallas kernels: 43.2 us -> 37.3 us  [per_device(): pl.pallas_call(functools.partial(gram_kernel, n_orig, n_link, cuts), out_...]
where the time goes in v1:
time: 42.4 us; the launch traced here: 42.3 us
  Pallas kernels  42.3 us (100%)
    pallas_call x1, Pallas kernels, per_device(): pl.pallas_call(functools.partial(gram_kernel, n_orig, n_link, cuts), out_...  37.3 us
    pallas_call x1, Pallas kernels, per_device(): pl.pallas_call(update_kernel, out_shape=jax.ShapeDtypeStruct((own_rows, m...  4.97 us

profile of v1, /device:TPU:0, one launch (start us, length us, event | category | flops | bytes accessed | tf_op | source)
XLA Modules:
  0.0 42.3 jit_solution(2298655050027421159)
XLA Ops:
  0.0 37.3 %shard_map.73.final_ref = f32[256,256]{1,0:T(8,128)} custom-call(s32[12,1,16]{2,1,0:T(1,128)} %bitcast.4, s32[12,1,16]{2,1,0:T(1,128)} %bitcast.5, s32[16]{0:T(128)} %counts_ref.3, bf16[32,128,128]{2,1,0:T(8,128)(2,1)} %bitcast.3, bf16[2048,256]{1,0:T(8,128)(2,1)} %states_hbm.3, f32[1,128]{1,0:T(1,128)} %obs_ref.1, f32[1,128]{1,0:T(1,128)} %var_ref.1), custom_call_target="tpu_custom_call" | custom-call | tf_op jit(solution)/shard_map/pallas_call | solution.py:458
  37.3 5.0 %shard_map.74 = bf16[512,256]{1,0:T(8,128)(2,1)} custom-call(s32[16]{0:T(128)} %counts_ref.3, f32[256,256]{1,0:T(8,128)} %shard_map.73.final_ref, bf16[2048,256]{1,0:T(8,128)(2,1)} %states_hbm.3), custom_call_target="tpu_custom_call" | custom-call | tf_op jit(solution)/shard_map/pallas_call | solution.py:498

commit v2 on v1

--- a/solution.py
+++ b/solution.py
@@ -9,7 +9,7 @@
 
 NS_ITERS = 4
 CUTS = 4
-UNROLL = 2
+SPAN = 8
 WIDE_GRANT = 67043328 - 900 * 1024
 MESH = pl.DeviceIdType.MESH
 F32 = jnp.float32
@@ -47,82 +47,91 @@
     ) + jnp.dot(a_high, b_high, preferred_element_type=F32)
 
 
-def sort_slots(ids_ref, targets_ref, words_ref, bits):
+def sort_slots(ids_ref, targets_ref, table_ref, tiles, link_blocks):
     slots = ids_ref.shape[0]
-    blocks = ids_ref.shape[2]
+    bits = max(1, (tiles - 1).bit_length())
     per_word = 31 // bits
-    n_words = pl.cdiv(slots, per_word)
-
-    def sort_block(block, carry):
-        amounts = [targets_ref[slot, 0, block] * 4 for slot in range(slots)]
-        ones = [jnp.left_shift(1, amount) for amount in amounts]
-        tally = functools.reduce(lambda a, b: a + b, ones)
-        starts = jnp.int32(0)
-        for shift in range(1, 8):
-            starts = starts + jnp.left_shift(tally, 4 * shift)
-        place = starts
-        words = [jnp.int32(0) for _ in range(n_words)]
+    targets = [targets_ref[slot] for slot in range(slots)]
+    ones = [jnp.left_shift(jnp.ones_like(target), target * 4) for target in targets]
+    tally = functools.reduce(lambda a, b: a + b, ones)
+    starts = jnp.zeros_like(tally)
+    for shift in range(1, 8):
+        starts = starts + jnp.left_shift(tally, jnp.full_like(tally, 4 * shift))
+    place = starts
+    words = [jnp.zeros_like(tally) for _ in range(pl.cdiv(slots, per_word))]
+    for slot in range(slots):
+        rank = jnp.bitwise_and(jnp.right_shift(place, targets[slot] * 4), 15)
+        place = place + ones[slot]
+        tile = ids_ref[slot]
+        for word in range(len(words)):
+            local = rank - word * per_word
+            inside = (local >= 0) & (local < per_word)
+            shifted = jnp.left_shift(tile, jnp.where(inside, local * bits, 0))
+            words[word] = words[word] + jnp.where(inside, shifted, 0)
+    rows = []
+    for slot in range(slots):
+        amount = jnp.full_like(tally, slot % per_word * bits)
+        rows.append(jnp.bitwise_and(jnp.right_shift(words[slot // per_word], amount), 2**bits - 1))
+    for target in range(1, link_blocks):
+        rows.append(jnp.bitwise_and(jnp.right_shift(starts, jnp.full_like(tally, 4 * target)), 15))
+    for index, row in enumerate(rows):
+        table_ref[index : index + 1, 0 : row.shape[1]] = row
+
+
+def build_group(table_ref, tiles_ref, prefix_refs, lhs_ref, group, cut_index, slots, link_blocks):
+    tiles, cut_rows, block_rows = tiles_ref.shape[1:]
+    span = lhs_ref.shape[0] // 2
+    for index in range(span):
+        prefix_ref = prefix_refs[index % len(prefix_refs)]
+        block = group * span + index
+        total = jnp.zeros((cut_rows, block_rows), F32)
         for slot in range(slots):
-            rank = jnp.bitwise_and(jnp.right_shift(place, amounts[slot]), 15)
-            place = place + ones[slot]
-            tile = ids_ref[slot, 0, block]
-            for word in range(n_words):
-                local = rank - word * per_word
-                inside = (local >= 0) & (local < per_word)
-                shift = jnp.where(inside, local * bits, 0)
-                words[word] = words[word] + jnp.where(inside, jnp.left_shift(tile, shift), 0)
-        words_ref[0, block] = starts
-        words_ref[1, block] = place
-        for word in range(n_words):
-            words_ref[2 + word, block] = words[word]
+            tile = table_ref[slot, block]
+            total = total + tiles_ref[cut_index, tile].astype(F32)
+            prefix_ref[slot + 1] = total
+        before = None
+        for target in range(link_blocks):
+            upto = total
+            if target < link_blocks - 1:
+                end = table_ref[slots + target, block]
+                upto = prefix_ref[end]
+            high, low = split(upto if before is None else upto - before)
+            before = upto
+            rows = slice(target * cut_rows, (target + 1) * cut_rows)
+            lhs_ref[index, rows] = high
+            lhs_ref[span + index, rows] = low
+
+
+def predict_cut(table_ref, tiles_ref, states_ref, prefix_refs, lhs_ref, term_ref, cut_index, cuts, slots):
+    cut_rows, block_rows = tiles_ref.shape[2:]
+    link_rows = cut_rows * cuts
+    link_blocks = term_ref.shape[0] // link_rows
+    span = lhs_ref.shape[0] // 2
+    depth = span * block_rows
+    groups = states_ref.shape[0] // depth
+
+    def rows_of(target):
+        return pl.ds(target * link_rows + cut_index * cut_rows, cut_rows)
+
+    def build(place):
+        cut_at = jnp.minimum(place // groups, cuts - 1)
+        build_group(table_ref, tiles_ref, prefix_refs, lhs_ref, place % groups, cut_at, slots, link_blocks)
+
+    for target in range(link_blocks):
+        term_ref[rows_of(target)] = jnp.zeros((cut_rows, term_ref.shape[1]), F32)
+    if cut_index == 0:
+        build(0)
+
+    def add_group(group, carry):
+        states = states_ref[pl.ds(pl.multiple_of(group * depth, depth), depth)]
+        left = jnp.concatenate([lhs_ref[index] for index in range(2 * span)], axis=1)
+        product = jnp.dot(left, jnp.concatenate([states, states], axis=0), preferred_element_type=F32)
+        build(cut_index * groups + group + 1)
+        for target in range(link_blocks):
+            term_ref[rows_of(target)] = term_ref[rows_of(target)] + product[target * cut_rows : (target + 1) * cut_rows]
         return carry
 
-    lax.fori_loop(0, blocks, sort_block, 0)
-
-
-def predict_cut(words_ref, tiles_ref, states_ref, prefix_refs, term_ref, cut_index, cut_rows, slots, bits):
-    link_rows, block_rows = tiles_ref.shape[1:]
-    link_blocks = term_ref.shape[0] // link_rows
-    per_word = 31 // bits
-    span = len(prefix_refs)
-    steps = states_ref.shape[0] // (span * block_rows)
-    rows_at = pl.ds(cut_index * cut_rows, cut_rows)
-
-    def add_step(step, carry):
-        highs, lows = [], []
-        for index, prefix_ref in enumerate(prefix_refs):
-            block = step * span + index
-            words = [words_ref[2 + word, block] for word in range(pl.cdiv(slots, per_word))]
-            total = jnp.zeros((cut_rows, block_rows), F32)
-            for slot in range(slots):
-                shifted = jnp.right_shift(words[slot // per_word], slot % per_word * bits)
-                tile = jnp.bitwise_and(shifted, 2**bits - 1)
-                total = total + tiles_ref[tile, rows_at, :].astype(F32)
-                prefix_ref[slot + 1, 0:cut_rows] = total
-            starts, ends = words_ref[0, block], words_ref[1, block]
-            high_parts, low_parts = [], []
-            for target in range(link_blocks):
-                first = jnp.bitwise_and(jnp.right_shift(starts, 4 * target), 15)
-                last = jnp.bitwise_and(jnp.right_shift(ends, 4 * target), 15)
-                high, low = split(prefix_ref[last, 0:cut_rows] - prefix_ref[first, 0:cut_rows])
-                high_parts.append(high)
-                low_parts.append(low)
-            highs.append(jnp.concatenate(high_parts, axis=0))
-            lows.append(jnp.concatenate(low_parts, axis=0))
-        states = states_ref[pl.ds(pl.multiple_of(step * span * block_rows, span * block_rows), span * block_rows)]
-        product = jnp.dot(jnp.concatenate(highs, axis=1), states, preferred_element_type=F32) + jnp.dot(
-            jnp.concatenate(lows, axis=1), states, preferred_element_type=F32
-        )
-        for target in range(link_blocks):
-            where = pl.ds(target * link_rows + cut_index * cut_rows, cut_rows)
-            term_ref[where] = term_ref[where] + product[target * cut_rows : (target + 1) * cut_rows]
-        return carry
-
-    for target in range(link_blocks):
-        term_ref[pl.ds(target * link_rows + cut_index * cut_rows, cut_rows)] = jnp.zeros(
-            (cut_rows, term_ref.shape[1]), F32
-        )
-    lax.fori_loop(0, steps, add_step, 0, unroll=UNROLL)
+    lax.fori_loop(0, groups, add_group, 0)
 
 
 def transform_of(gram, forcing):
@@ -149,7 +158,7 @@
 
 def gram_kernel(
     n_orig, n_link, cuts, ids_ref, targets_ref, counts_ref, tiles_hbm, states_hbm, obs_ref, var_ref, out_ref,
-    tiles_ref, states_ref, tiles_sem, states_sem, even_ref, odd_ref, words_ref, term_ref, first_in, sums, side_in, far_in, gram_ref, half_in, half_ref, piece_in, piece_ref, final_ref,
+    tiles_ref, states_ref, tiles_sem, states_sem, even_ref, odd_ref, lhs_ref, packed_ref, table_ref, table_sem, term_ref, first_in, sums, side_in, far_in, gram_ref, half_in, half_ref, piece_in, piece_ref, final_ref,
     send1, recv1, send2, recv2, send7, recv7, send3, recv3, send4, recv4, send5, recv5, send6, recv6,
 ):
     orig = lax.axis_index("orig")
@@ -173,8 +182,15 @@
 
     load_states = pltpu.make_async_copy(states_hbm, states_ref, states_sem)
     load_states.start()
-    load_tiles = pltpu.make_async_copy(tiles_hbm, tiles_ref, tiles_sem)
-    load_tiles.start()
+
+    def load_tiles(index):
+        part = tiles_ref.shape[2]
+        return pltpu.make_async_copy(
+            tiles_hbm.at[:, pl.ds(index * part, part)], tiles_ref.at[index], tiles_sem.at[index]
+        )
+
+    for index in range(cuts):
+        load_tiles(index).start()
     near = place % 2
     far = place // 2
     n_far = pairs // 2
@@ -191,8 +207,10 @@
     slots = ids_ref.shape[0]
     blocks = counts_ref.shape[0]
     block_rows = states_ref.shape[0] // blocks
-    bits = max(1, (tiles_ref.shape[0] - 1).bit_length())
-    sort_slots(ids_ref, targets_ref, words_ref, bits)
+    link_rows = tiles_ref.shape[2] * cuts
+    sort_slots(ids_ref, targets_ref, packed_ref, tiles_ref.shape[1], rows * n_orig // link_rows)
+    move_table = pltpu.make_async_copy(packed_ref, table_ref, table_sem)
+    move_table.start()
     for prefix_ref in (even_ref, odd_ref):
         prefix_ref[...] = jnp.zeros(prefix_ref.shape, F32)
     position = lax.broadcasted_iota(jnp.int32, (block_rows, members), 0)
@@ -205,7 +223,9 @@
         return carry
 
     lax.fori_loop(0, blocks, mask_block, 0, unroll=2)
-    load_tiles.wait()
+    for index in range(cuts):
+        load_tiles(index).wait()
+    move_table.wait()
 
     cut_rows = rows // cuts
     steps = n_far * cuts
@@ -251,8 +271,7 @@
 
     for index in range(cuts):
         predict_cut(
-            words_ref, tiles_ref, states_ref, (even_ref, odd_ref), term_ref,
-            index, tiles_ref.shape[1] // cuts, slots, bits,
+            table_ref, tiles_ref, states_ref, (even_ref, odd_ref), lhs_ref, term_ref, index, cuts, slots
         )
         if index == 0:
             pl.semaphore_wait(barrier, n_far + n_link)
@@ -454,20 +473,24 @@
     piece = half // min(ring, half // 8)
     cuts = CUTS if rows == link_rows else 1
     slots = pattern_ids.shape[2]
+    table_rows = pl.cdiv(slots + link_blocks, 8) * 8
     steps = pairs // 2 * cuts
     gram = pl.pallas_call(
         functools.partial(gram_kernel, n_orig, n_link, cuts),
         out_shape=jax.ShapeDtypeStruct((members, members), F32),
-        in_specs=[smem, smem, smem, hbm, hbm, vmem, vmem],
+        in_specs=[vmem, vmem, smem, hbm, hbm, vmem, vmem],
         out_specs=vmem,
         scratch_shapes=[
-            pltpu.VMEM(patterns.shape[1:], BF16),
+            pltpu.VMEM((cuts, patterns.shape[1], link_rows // cuts, block_rows), BF16),
             pltpu.VMEM((states_dev, members), BF16),
-            dma,
+            dma((cuts,)),
             dma,
             pltpu.VMEM((16, link_rows // cuts, block_rows), F32),
             pltpu.VMEM((16, link_rows // cuts, block_rows), F32),
-            pltpu.SMEM((8, blocks_dev), jnp.int32),
+            pltpu.VMEM((2 * SPAN, link_blocks * link_rows // cuts, block_rows), BF16),
+            pltpu.VMEM((table_rows, 128), jnp.int32),
+            pltpu.SMEM((table_rows, 128), jnp.int32),
+            dma,
             pltpu.VMEM((link_blocks * link_rows, members), F32),
             pltpu.VMEM((pairs, rows, members), F32),
             pltpu.VMEM((pairs, rows, members), F32),

time: 42.4 us -> 41.1 us (0.969)
  Pallas kernels: 42.3 us -> 40.8 us
    pallas_call x1, Pallas kernels: 37.3 us -> 35.9 us  [per_device(): pl.pallas_call(functools.partial(gram_kernel, n_orig, n_link, cuts), out_...]
where the time goes in v2:
time: 41.1 us; the launch traced here: 40.8 us
  Pallas kernels  40.8 us (99%)
    pallas_call x1, Pallas kernels, per_device(): pl.pallas_call(functools.partial(gram_kernel, n_orig, n_link, cuts), out_...  35.9 us
    pallas_call x1, Pallas kernels, per_device(): pl.pallas_call(update_kernel, out_shape=jax.ShapeDtypeStruct((own_rows, m...  4.97 us

profile of v2, /device:TPU:0, one launch (start us, length us, event | category | flops | bytes accessed | tf_op | source)
XLA Modules:
  0.0 40.8 jit_solution(17186098688039006451)
XLA Ops:
  0.0 35.9 %shard_map.73.final_ref = f32[256,256]{1,0:T(8,128)} custom-call(s32[12,1,16]{2,1,0:T(1,128)} %bitcast.4, s32[12,1,16]{2,1,0:T(1,128)} %bitcast.5, s32[16]{0:T(128)} %counts_ref.3, bf16[32,128,128]{2,1,0:T(8,128)(2,1)} %bitcast.3, bf16[2048,256]{1,0:T(8,128)(2,1)} %states_hbm.3, f32[1,128]{1,0:T(1,128)} %obs_ref.1, f32[1,128]{1,0:T(1,128)} %var_ref.1), custom_call_target="tpu_custom_call" | custom-call | tf_op jit(solution)/shard_map/pallas_call | solution.py:478
  35.9 5.0 %shard_map.74 = bf16[512,256]{1,0:T(8,128)(2,1)} custom-call(s32[16]{0:T(128)} %counts_ref.3, f32[256,256]{1,0:T(8,128)} %shard_map.73.final_ref, bf16[2048,256]{1,0:T(8,128)(2,1)} %states_hbm.3), custom_call_target="tpu_custom_call" | custom-call | tf_op jit(solution)/shard_map/pallas_call | solution.py:521

commit v3 on v2

--- a/solution.py
+++ b/solution.py
@@ -10,7 +10,7 @@
 NS_ITERS = 4
 CUTS = 4
 SPAN = 8
-WIDE_GRANT = 67043328 - 900 * 1024
+WIDE_GRANT = 67043328-900*1024
 MESH = pl.DeviceIdType.MESH
 F32 = jnp.float32
 BF16 = jnp.bfloat16
@@ -134,6 +134,11 @@
     lax.fori_loop(0, groups, add_group, 0)
 
 
+def column_of(row):
+    width = row.shape[1]
+    return jnp.broadcast_to(row, (width, width)).T
+
+
 def transform_of(gram, forcing):
     members = gram.shape[0]
     row = lax.broadcasted_iota(jnp.int32, (members, members), 0)
@@ -150,15 +155,15 @@
         if sweep < NS_ITERS - 1:
             root = mm3(root, middle)
         inverse = mm3(middle, inverse)
-    inner = mm3(jnp.broadcast_to(forcing, (8, members)), inverse)
-    mean_weights = mm3(inner, inverse)[0:1] / (bound * (members - 1.0))
-    whole = inverse / jnp.sqrt(bound) + jnp.broadcast_to(mean_weights, (members, members)).T
+    inner = jnp.sum(inverse * column_of(forcing), axis=0, keepdims=True)
+    mean_weights = jnp.sum(inverse * inner, axis=1, keepdims=True) / (bound * (members - 1.0))
+    whole = inverse / jnp.sqrt(bound) + mean_weights
     return whole + (1.0 - jnp.sum(whole, axis=0, keepdims=True)) / members
 
 
 def gram_kernel(
-    n_orig, n_link, cuts, ids_ref, targets_ref, counts_ref, tiles_hbm, states_hbm, obs_ref, var_ref, out_ref,
-    tiles_ref, states_ref, tiles_sem, states_sem, even_ref, odd_ref, lhs_ref, packed_ref, table_ref, table_sem, term_ref, first_in, sums, side_in, far_in, gram_ref, half_in, half_ref, piece_in, piece_ref, final_ref,
+    n_orig, n_link, cuts, ids_hbm, targets_hbm, counts_hbm, tiles_hbm, states_hbm, obs_hbm, var_hbm, out_ref,
+    ids_ref, targets_ref, counts_ref, obs_ref, var_ref, small_sem, tiles_ref, states_ref, tiles_sem, states_sem, even_ref, odd_ref, lhs_ref, packed_ref, table_ref, table_sem, term_ref, first_in, sums, side_in, far_in, gram_ref, half_in, half_ref, piece_in, piece_ref, final_ref,
     send1, recv1, send2, recv2, send7, recv7, send3, recv3, send4, recv4, send5, recv5, send6, recv6,
 ):
     orig = lax.axis_index("orig")
@@ -180,6 +185,17 @@
     def device_of(other):
         return (other % n_orig, (other // n_orig) * 2 + side)
 
+    load_small = [
+        pltpu.make_async_copy(source, target, small_sem.at[index])
+        for index, (source, target) in enumerate(
+            [
+                (ids_hbm, ids_ref), (targets_hbm, targets_ref), (counts_hbm, counts_ref),
+                (obs_hbm, obs_ref), (var_hbm, var_ref),
+            ]
+        )
+    ]
+    for copy in load_small[:3]:
+        copy.start()
     load_states = pltpu.make_async_copy(states_hbm, states_ref, states_sem)
     load_states.start()
 
@@ -191,6 +207,8 @@
 
     for index in range(cuts):
         load_tiles(index).start()
+    for copy in load_small[3:]:
+        copy.start()
     near = place % 2
     far = place // 2
     n_far = pairs // 2
@@ -208,12 +226,15 @@
     blocks = counts_ref.shape[0]
     block_rows = states_ref.shape[0] // blocks
     link_rows = tiles_ref.shape[2] * cuts
+    load_small[0].wait()
+    load_small[1].wait()
     sort_slots(ids_ref, targets_ref, packed_ref, tiles_ref.shape[1], rows * n_orig // link_rows)
     move_table = pltpu.make_async_copy(packed_ref, table_ref, table_sem)
     move_table.start()
     for prefix_ref in (even_ref, odd_ref):
         prefix_ref[...] = jnp.zeros(prefix_ref.shape, F32)
     position = lax.broadcasted_iota(jnp.int32, (block_rows, members), 0)
+    load_small[2].wait()
     load_states.wait()
 
     def mask_block(block, carry):
@@ -325,6 +346,8 @@
 
     repeat(remote, gather)
 
+    load_small[3].wait()
+    load_small[4].wait()
     predicted = sums[pairs - 1]
     turned = predicted.T
     weights = 1.0 / var_ref[...]
@@ -422,14 +445,16 @@
     share.wait_send()
 
 
-def update_kernel(counts_ref, final_ref, states_hbm, out_ref, states_ref, states_sem):
+def update_kernel(counts_hbm, final_ref, states_hbm, out_hbm, counts_ref, states_ref, done_ref, counts_sem, states_sem, done_sem):
     link = lax.axis_index("link")
-    own_rows, members = out_ref.shape
+    own_rows, members = done_ref.shape
     half = members // 2
     fetch = pltpu.make_async_copy(
         states_hbm.at[pl.ds(pl.multiple_of(link * own_rows, own_rows), own_rows)], states_ref, states_sem
     )
     fetch.start()
+    fetch_counts = pltpu.make_async_copy(counts_hbm, counts_ref, counts_sem)
+    fetch_counts.start()
     upper = final_ref[0:half, half:]
     gram = jnp.concatenate(
         [final_ref[0:half, :], jnp.concatenate([upper.T, final_ref[half:, half:]], axis=1)], axis=0
@@ -439,18 +464,27 @@
     )
     high, low = split(transform_of(gram, forcing))
     fetch.wait()
+    fetch_counts.wait()
     block_rows = states_hbm.shape[0] // counts_ref.shape[0]
     blocks = own_rows // block_rows
     position = lax.broadcasted_iota(jnp.int32, (block_rows, members), 0)
+
+    def store(index):
+        where = slice(index * block_rows, (index + 1) * block_rows)
+        return pltpu.make_async_copy(done_ref.at[where], out_hbm.at[where], done_sem.at[index])
+
     for index in range(blocks):
         states = states_ref[index * block_rows : (index + 1) * block_rows]
         updated = jnp.dot(states, low, preferred_element_type=F32) + jnp.dot(
             states, high, preferred_element_type=F32
         )
         living = position < counts_ref[link * blocks + index]
-        out_ref[index * block_rows : (index + 1) * block_rows] = jnp.where(
+        done_ref[index * block_rows : (index + 1) * block_rows] = jnp.where(
             living, updated, states.astype(F32)
         ).astype(BF16)
+        store(index).start()
+    for index in range(blocks):
+        store(index).wait()
 
 
 def per_device(background, live_counts, patterns, pattern_ids, link_targets, counts_obs, obs_var):
@@ -463,7 +497,6 @@
     rows = counts_obs.shape[1]
     link_blocks = rows * n_orig // link_rows
     vmem = pl.BlockSpec(memory_space=pltpu.VMEM)
-    smem = pl.BlockSpec(memory_space=pltpu.SMEM)
     hbm = pl.BlockSpec(memory_space=pl.ANY)
     dma = pltpu.SemaphoreType.DMA
     grant = pltpu.CompilerParams(vmem_limit_bytes=WIDE_GRANT)
@@ -477,10 +510,16 @@
     steps = pairs // 2 * cuts
     gram = pl.pallas_call(
         functools.partial(gram_kernel, n_orig, n_link, cuts),
-        out_shape=jax.ShapeDtypeStruct((members, members), F32),
-        in_specs=[vmem, vmem, smem, hbm, hbm, vmem, vmem],
+        out_shape=pltpu.VMEM((members, members), F32),
+        in_specs=[hbm] * 7,
         out_specs=vmem,
         scratch_shapes=[
+            pltpu.VMEM((slots, 1, blocks_dev), jnp.int32),
+            pltpu.VMEM((slots, 1, blocks_dev), jnp.int32),
+            pltpu.SMEM((blocks_dev,), jnp.int32),
+            pltpu.VMEM((1, rows), F32),
+            pltpu.VMEM((1, rows), F32),
+            dma((5,)),
             pltpu.VMEM((cuts, patterns.shape[1], link_rows // cuts, block_rows), BF16),
             pltpu.VMEM((states_dev, members), BF16),
             dma((cuts,)),
@@ -521,11 +560,18 @@
     return pl.pallas_call(
         update_kernel,
         out_shape=jax.ShapeDtypeStruct((own_rows, members), BF16),
-        in_specs=[smem, vmem, hbm],
-        out_specs=vmem,
-        scratch_shapes=[pltpu.VMEM((own_rows, members), BF16), dma],
+        in_specs=[hbm, vmem, hbm],
+        out_specs=hbm,
+        scratch_shapes=[
+            pltpu.SMEM((blocks_dev,), jnp.int32),
+            pltpu.VMEM((own_rows, members), BF16),
+            pltpu.VMEM((own_rows, members), BF16),
+            dma,
+            dma,
+            dma((own_rows // block_rows,)),
+        ],
         compiler_params=grant,
-    )(live_counts, gram, background)
+    )(live_counts, pltpu.with_memory_space_constraint(gram, pltpu.VMEM), background)
 
 
 def solution(mesh):

time: 41.1 us -> 39 us (0.949)
  Pallas kernels: 40.8 us -> 38.8 us
    pallas_call x1, Pallas kernels: 35.9 us -> 34.6 us  [per_device(): pl.pallas_call(functools.partial(gram_kernel, n_orig, n_link, cuts), out_...]
    pallas_call x1, Pallas kernels: 4.97 us -> 4.23 us  [per_device(): pl.pallas_call(update_kernel, out_shape=jax.ShapeDtypeStruct((own_rows, m...]
where the time goes in v3:
time: 39 us; the launch traced here: 38.8 us
  Pallas kernels  38.8 us (99%)
    pallas_call x1, Pallas kernels, per_device(): pl.pallas_call(functools.partial(gram_kernel, n_orig, n_link, cuts), out_...  34.6 us
    pallas_call x1, Pallas kernels, per_device(): pl.pallas_call(update_kernel, out_shape=jax.ShapeDtypeStruct((own_rows, m...  4.23 us

profile of v3, /device:TPU:0, one launch (start us, length us, event | category | flops | bytes accessed | tf_op | source)
XLA Modules:
  0.0 38.8 jit_solution(12126903298223127033)
XLA Ops:
  0.0 34.6 %shard_map.73.final_ref = f32[256,256]{1,0:T(8,128)S(1)} custom-call(s32[12,1,16]{2,1,0:T(1,128)} %bitcast.4, s32[12,1,16]{2,1,0:T(1,128)} %bitcast.5, s32[16]{0:T(128)} %counts_hbm.3, bf16[32,128,128]{2,1,0:T(8,128)(2,1)} %bitcast.3, bf16[2048,256]{1,0:T(8,128)(2,1)} %states_hbm.3, f32[1,128]{1,0:T(1,128)} %obs_hbm.1, f32[1,128]{1,0:T(1,128)} %var_hbm.1), custom_call_target="tpu_custom_call" | custom-call | tf_op jit(solution)/shard_map/pallas_call | solution.py:511
  34.6 4.2 %shard_map.74 = bf16[512,256]{1,0:T(8,128)(2,1)} custom-call(s32[16]{0:T(128)} %counts_hbm.3, f32[256,256]{1,0:T(8,128)S(1)} %shard_map.73.final_ref, bf16[2048,256]{1,0:T(8,128)(2,1)} %states_hbm.3), custom_call_target="tpu_custom_call" | custom-call | tf_op jit(solution)/shard_map/pallas_call | solution.py:560

commit v4 on v3

--- a/solution.py
+++ b/solution.py
@@ -41,10 +41,15 @@
 def mm3(a, b):
     a_high, a_low = split(a)
     b_high, b_low = split(b)
-    return (
-        jnp.dot(a_high, b_low, preferred_element_type=F32)
-        + jnp.dot(a_low, b_high, preferred_element_type=F32)
-    ) + jnp.dot(a_high, b_high, preferred_element_type=F32)
+    left = jnp.concatenate([a_high, a_low, a_high], axis=1)
+    right = jnp.concatenate([b_low, b_high, b_high], axis=0)
+    height = left.shape[0] // 2
+    if height % 16:
+        return jnp.dot(left, right, preferred_element_type=F32)
+    return jnp.concatenate(
+        [jnp.dot(left[0:height], right, preferred_element_type=F32), jnp.dot(left[height:], right, preferred_element_type=F32)],
+        axis=0,
+    )
 
 
 def sort_slots(ids_ref, targets_ref, table_ref, tiles, link_blocks):
@@ -354,32 +359,40 @@
     mean_row = jnp.sum(turned, axis=0, keepdims=True) / members
     spread = predicted - jnp.sum(predicted, axis=1, keepdims=True) / members
     spread_t = turned - mean_row
-    gram_ref[...] = mm3(spread_t * weights, spread)
+    gram = mm3(spread_t * weights, spread)
     pull = jnp.broadcast_to(weights * (obs_ref[...] - mean_row), (8, rows))
     forcing = mm3(pull, spread)
-    gram_ref[pl.ds(half, 1), 0:half] = forcing[0:1, 0:half]
-    gram_ref[pl.ds(half + 1, 1), 0:half] = forcing[0:1, half:]
+    row = lax.broadcasted_iota(jnp.int32, (half, half), 0)
+    column = lax.broadcasted_iota(jnp.int32, (half, half), 1)
+    corner = gram[half:, half:]
+    halves = (gram[0:half, half:], jnp.where(row <= column, gram[0:half, 0:half], corner))
+    diagonal = jnp.sum(jnp.where(row == column, corner, 0.0), axis=0, keepdims=True)
+    extras = (forcing[0:1, 0:half], forcing[0:1, half:], diagonal)
+    for which, values in enumerate(halves):
+        for index in range(owners):
+            gram_ref[which, index, 0:piece] = values[index * piece : (index + 1) * piece]
+            extra = extras[index] if which == 0 and index < len(extras) else jnp.zeros((1, half), F32)
+            gram_ref[which, index, pl.ds(piece, 1)] = extra
 
     swap = pltpu.make_async_remote_copy(
-        src_ref=gram_ref.at[pl.ds(pl.multiple_of((1 - side) * half, half), half)], dst_ref=half_in,
+        src_ref=gram_ref.at[1 - side], dst_ref=half_in,
         send_sem=send3, recv_sem=recv3, device_id=(orig, twin), device_id_type=MESH,
     )
     swap.start()
     swap.wait_recv()
-    half_ref[...] = gram_ref[pl.ds(pl.multiple_of(side * half, half), half)] + half_in[...]
+    half_ref[...] = gram_ref[side] + half_in[...]
 
     def scatter(step):
         other = xor(rank, ring - 1 - step, ring)
         return pltpu.make_async_remote_copy(
-            src_ref=half_ref.at[pl.ds(pl.multiple_of(other * piece, piece), piece)], dst_ref=piece_in.at[step],
+            src_ref=half_ref.at[other], dst_ref=piece_in.at[step],
             send_sem=send4.at[step], recv_sem=recv4.at[step],
             device_id=device_of(other), device_id_type=MESH,
         )
 
     def spread_out(source, step, other):
-        where = pl.ds(pl.multiple_of(side * half + source * piece, piece), piece)
         return pltpu.make_async_remote_copy(
-            src_ref=piece_ref, dst_ref=final_ref.at[where],
+            src_ref=piece_ref, dst_ref=final_ref.at[side, source],
             send_sem=send5.at[step], recv_sem=recv5.at[step],
             device_id=device_of(other), device_id_type=MESH,
         )
@@ -396,7 +409,7 @@
     repeat(ring - 1, scatter_start)
 
     def reduce_piece():
-        piece_ref[...] = half_ref[pl.ds(pl.multiple_of(rank * piece, piece), piece)]
+        piece_ref[...] = half_ref[rank]
 
         def add(step):
             scatter(step).wait_recv()
@@ -404,7 +417,7 @@
 
         repeat(ring - 1, add)
         repeat(ring - 1, lambda step: spread_out(rank, step, xor(rank, ring - 1 - step, ring)).start())
-        final_ref[pl.ds(pl.multiple_of(side * half + rank * piece, piece), piece)] = piece_ref[...]
+        final_ref[side, rank] = piece_ref[...]
 
     guarded(rank < owners, reduce_piece)
 
@@ -413,9 +426,8 @@
         guarded(other < owners, lambda: spread_out(other, step, other).wait_recv())
 
     repeat(ring - 1, spread_wait)
-    mine = pl.ds(pl.multiple_of(side * half, half), half)
     share = pltpu.make_async_remote_copy(
-        src_ref=final_ref.at[mine], dst_ref=final_ref.at[mine],
+        src_ref=final_ref.at[side], dst_ref=final_ref.at[side],
         send_sem=send6, recv_sem=recv6, device_id=(orig, twin), device_id_type=MESH,
     )
     share.start()
@@ -455,13 +467,21 @@
     fetch.start()
     fetch_counts = pltpu.make_async_copy(counts_hbm, counts_ref, counts_sem)
     fetch_counts.start()
-    upper = final_ref[0:half, half:]
+    owners = final_ref.shape[1]
+    piece = half // owners
+    upper, mixed = [
+        jnp.concatenate([final_ref[which, index, 0:piece] for index in range(owners)], axis=0) for which in range(2)
+    ]
+    first, second, diagonal = [final_ref[0, index, pl.ds(piece, 1)] for index in range(3)]
+    row = lax.broadcasted_iota(jnp.int32, (half, half), 0)
+    column = lax.broadcasted_iota(jnp.int32, (half, half), 1)
+    turned = mixed.T
+    head = jnp.where(row <= column, mixed, turned)
+    tail = jnp.where(row == column, diagonal, jnp.where(row > column, mixed, turned))
     gram = jnp.concatenate(
-        [final_ref[0:half, :], jnp.concatenate([upper.T, final_ref[half:, half:]], axis=1)], axis=0
-    )
-    forcing = jnp.concatenate(
-        [final_ref[pl.ds(half, 1), 0:half], final_ref[pl.ds(half + 1, 1), 0:half]], axis=1
-    )
+        [jnp.concatenate([head, upper], axis=1), jnp.concatenate([upper.T, tail], axis=1)], axis=0
+    )
+    forcing = jnp.concatenate([first, second], axis=1)
     high, low = split(transform_of(gram, forcing))
     fetch.wait()
     fetch_counts.wait()
@@ -503,14 +523,15 @@
     pairs = n_orig // 2
     ring = n_orig * n_link // 2
     half = members // 2
-    piece = half // min(ring, half // 8)
+    owners = min(ring, half // 8)
+    packed = (owners, half // owners + 1, half)
     cuts = CUTS if rows == link_rows else 1
     slots = pattern_ids.shape[2]
     table_rows = pl.cdiv(slots + link_blocks, 8) * 8
     steps = pairs // 2 * cuts
     gram = pl.pallas_call(
         functools.partial(gram_kernel, n_orig, n_link, cuts),
-        out_shape=pltpu.VMEM((members, members), F32),
+        out_shape=pltpu.VMEM((2,) + packed, F32),
         in_specs=[hbm] * 7,
         out_specs=vmem,
         scratch_shapes=[
@@ -535,12 +556,12 @@
             pltpu.VMEM((pairs, rows, members), F32),
             pltpu.VMEM((pairs // 2, rows, members), F32),
             pltpu.VMEM((pairs // 2, rows, members), F32),
-            pltpu.VMEM((members, members), F32),
-            pltpu.VMEM((half, members), F32),
-            pltpu.VMEM((half, members), F32),
-            pltpu.VMEM((ring - 1, piece, members), F32),
-            pltpu.VMEM((piece, members), F32),
-            pltpu.VMEM((members, members), F32),
+            pltpu.VMEM((2,) + packed, F32),
+            pltpu.VMEM(packed, F32),
+            pltpu.VMEM(packed, F32),
+            pltpu.VMEM((ring - 1,) + packed[1:], F32),
+            pltpu.VMEM(packed[1:], F32),
+            pltpu.VMEM((2,) + packed, F32),
             dma((2 * steps,)), dma((2 * steps,)),
             dma((steps,)), dma((steps,)),
             dma((steps,)), dma((steps,)),

time: 39 us -> 37.2 us (0.954)
  Pallas kernels: 38.8 us -> 37 us
    pallas_call x1, Pallas kernels: 34.6 us -> 33 us  [per_device(): pl.pallas_call(functools.partial(gram_kernel, n_orig, n_link, cuts), out_...]
where the time goes in v4:
time: 37.2 us; the launch traced here: 37 us
  Pallas kernels  37 us (99%)
    pallas_call x1, Pallas kernels, per_device(): pl.pallas_call(functools.partial(gram_kernel, n_orig, n_link, cuts), out_...  33 us
    pallas_call x1, Pallas kernels, per_device(): pl.pallas_call(update_kernel, out_shape=jax.ShapeDtypeStruct((own_rows, m...  3.98 us

profile of v4, /device:TPU:0, one launch (start us, length us, event | category | flops | bytes accessed | tf_op | source)
XLA Modules:
  0.0 37.0 jit_solution(16446113798672153427)
XLA Ops:
  0.0 33.0 %shard_map.73.final_ref = f32[2,16,9,128]{3,2,1,0:T(8,128)S(1)} custom-call(s32[12,1,16]{2,1,0:T(1,128)} %bitcast.4, s32[12,1,16]{2,1,0:T(1,128)} %bitcast.5, s32[16]{0:T(128)} %counts_hbm.3, bf16[32,128,128]{2,1,0:T(8,128)(2,1)} %bitcast.3, bf16[2048,256]{1,0:T(8,128)(2,1)} %states_hbm.3, f32[1,128]{1,0:T(1,128)} %obs_hbm.1, f32[1,128]{1,0:T(1,128)} %var_hbm.1), custom_call_target="tpu_custom_call" | custom-call | tf_op jit(solution)/shard_map/pallas_call | solution.py:532
  33.0 4.0 %shard_map.74 = bf16[512,256]{1,0:T(8,128)(2,1)} custom-call(s32[16]{0:T(128)} %counts_hbm.3, f32[2,16,9,128]{3,2,1,0:T(8,128)S(1)} %shard_map.73.final_ref, bf16[2048,256]{1,0:T(8,128)(2,1)} %states_hbm.3), custom_call_target="tpu_custom_call" | custom-call | tf_op jit(solution)/shard_map/pallas_call | solution.py:581

commit v5 on v4

--- a/solution.py
+++ b/solution.py
@@ -22,6 +22,10 @@
             body(step)
     else:
         lax.fori_loop(0, count, lambda step, carry: (body(step), carry)[1], 0)
+
+
+def rolled(count, body):
+    lax.fori_loop(0, count, lambda step, carry: (body(step), carry)[1], 0)
 
 
 def xor(a, b, size):
@@ -107,36 +111,38 @@
             lhs_ref[span + index, rows] = low
 
 
-def predict_cut(table_ref, tiles_ref, states_ref, prefix_refs, lhs_ref, term_ref, cut_index, cuts, slots):
-    cut_rows, block_rows = tiles_ref.shape[2:]
+def predict(table_ref, tiles_ref, states_ref, prefix_refs, lhs_ref, term_ref, slots, after_cut):
+    cuts, _, cut_rows, block_rows = tiles_ref.shape
     link_rows = cut_rows * cuts
     link_blocks = term_ref.shape[0] // link_rows
     span = lhs_ref.shape[0] // 2
     depth = span * block_rows
     groups = states_ref.shape[0] // depth
 
-    def rows_of(target):
-        return pl.ds(target * link_rows + cut_index * cut_rows, cut_rows)
-
     def build(place):
         cut_at = jnp.minimum(place // groups, cuts - 1)
         build_group(table_ref, tiles_ref, prefix_refs, lhs_ref, place % groups, cut_at, slots, link_blocks)
 
-    for target in range(link_blocks):
-        term_ref[rows_of(target)] = jnp.zeros((cut_rows, term_ref.shape[1]), F32)
-    if cut_index == 0:
-        build(0)
-
-    def add_group(group, carry):
+    build(0)
+
+    def add_group(place, carry):
+        group = place % groups
+        cut_index = place // groups
         states = states_ref[pl.ds(pl.multiple_of(group * depth, depth), depth)]
         left = jnp.concatenate([lhs_ref[index] for index in range(2 * span)], axis=1)
         product = jnp.dot(left, jnp.concatenate([states, states], axis=0), preferred_element_type=F32)
-        build(cut_index * groups + group + 1)
+        build(place + 1)
         for target in range(link_blocks):
-            term_ref[rows_of(target)] = term_ref[rows_of(target)] + product[target * cut_rows : (target + 1) * cut_rows]
+            where = pl.ds(pl.multiple_of(target * link_rows + cut_index * cut_rows, cut_rows), cut_rows)
+            term_ref[where] = term_ref[where] + product[target * cut_rows : (target + 1) * cut_rows]
+
+        @pl.when(group == groups - 1)
+        def _():
+            after_cut(cut_index)
+
         return carry
 
-    lax.fori_loop(0, groups, add_group, 0)
+    lax.fori_loop(0, groups * cuts, add_group, 0)
 
 
 def column_of(row):
@@ -144,7 +150,7 @@
     return jnp.broadcast_to(row, (width, width)).T
 
 
-def transform_of(gram, forcing):
+def transform_of(gram, forcing, root_ref, inverse_ref):
     members = gram.shape[0]
     row = lax.broadcasted_iota(jnp.int32, (members, members), 0)
     column = lax.broadcasted_iota(jnp.int32, (members, members), 1)
@@ -153,13 +159,20 @@
     bound = jnp.max(jnp.sum(jnp.abs(system), axis=1, keepdims=True), axis=0, keepdims=True)
     root = system / bound
     middle = 1.5 * identity - 0.5 * root
-    inverse = middle
-    root = mm3(root, middle)
-    for sweep in range(1, NS_ITERS):
+    inverse_ref[...] = middle
+    root_ref[...] = mm3(root, middle)
+
+    def sweep(index, carry):
+        root = root_ref[...]
+        inverse = inverse_ref[...]
         middle = 1.5 * identity - 0.5 * mm3(inverse, root)
-        if sweep < NS_ITERS - 1:
-            root = mm3(root, middle)
-        inverse = mm3(middle, inverse)
+        root_ref[...] = mm3(root, middle)
+        inverse_ref[...] = mm3(middle, inverse)
+        return carry
+
+    lax.fori_loop(1, NS_ITERS - 1, sweep, 0)
+    inverse = inverse_ref[...]
+    inverse = mm3(1.5 * identity - 0.5 * mm3(inverse, root_ref[...]), inverse)
     inner = jnp.sum(inverse * column_of(forcing), axis=0, keepdims=True)
     mean_weights = jnp.sum(inverse * inner, axis=1, keepdims=True) / (bound * (members - 1.0))
     whole = inverse / jnp.sqrt(bound) + mean_weights
@@ -239,6 +252,7 @@
     for prefix_ref in (even_ref, odd_ref):
         prefix_ref[...] = jnp.zeros(prefix_ref.shape, F32)
     position = lax.broadcasted_iota(jnp.int32, (block_rows, members), 0)
+    term_ref[...] = jnp.zeros_like(term_ref)
     load_small[2].wait()
     load_states.wait()
 
@@ -295,11 +309,9 @@
     remote = steps - cuts
     lag = min(2, remote, cuts)
 
-    for index in range(cuts):
-        predict_cut(
-            table_ref, tiles_ref, states_ref, (even_ref, odd_ref), lhs_ref, term_ref, index, cuts, slots
-        )
-        if index == 0:
+    def after_cut(index):
+        @pl.when(index == 0)
+        def _():
             pl.semaphore_wait(barrier, n_far + n_link)
 
         def first_start(step):
@@ -307,6 +319,8 @@
             first(step * cuts + index, 0).start()
 
         repeat(n_far - 1, first_start)
+
+    predict(table_ref, tiles_ref, states_ref, (even_ref, odd_ref), lhs_ref, term_ref, slots, after_cut)
     repeat(cuts, lambda step: first(step + remote, 1).start())
     repeat(cuts, lambda step: first(step + remote, 0).start())
 
@@ -409,13 +423,22 @@
     repeat(ring - 1, scatter_start)
 
     def reduce_piece():
-        piece_ref[...] = half_ref[rank]
-
-        def add(step):
+        def arrive(step):
             scatter(step).wait_recv()
-            piece_ref[...] = piece_ref[...] + piece_in[step]
-
-        repeat(ring - 1, add)
+            return piece_in[step]
+
+        if ring <= 16:
+            total = half_ref[rank]
+            for step in range(ring - 1):
+                total = total + arrive(step)
+            piece_ref[...] = total
+        else:
+            piece_ref[...] = half_ref[rank]
+
+            def add(step):
+                piece_ref[...] = piece_ref[...] + arrive(step)
+
+            repeat(ring - 1, add)
         repeat(ring - 1, lambda step: spread_out(rank, step, xor(rank, ring - 1 - step, ring)).start())
         final_ref[side, rank] = piece_ref[...]
 
@@ -440,24 +463,24 @@
         first(step, 0).wait_send()
         beside(step).wait_send()
 
-    repeat(steps, first_end)
-    repeat(remote, lambda step: beyond(step).wait_send())
+    rolled(steps, first_end)
+    rolled(remote, lambda step: beyond(step).wait_send())
     swap.wait_send()
 
     def scatter_end(step):
         guarded(xor(rank, ring - 1 - step, ring) < owners, lambda: scatter(step).wait_send())
 
-    repeat(ring - 1, scatter_end)
+    rolled(ring - 1, scatter_end)
     guarded(
         rank < owners,
-        lambda: repeat(
+        lambda: rolled(
             ring - 1, lambda step: spread_out(rank, step, xor(rank, ring - 1 - step, ring)).wait_send()
         ),
     )
     share.wait_send()
 
 
-def update_kernel(counts_hbm, final_ref, states_hbm, out_hbm, counts_ref, states_ref, done_ref, counts_sem, states_sem, done_sem):
+def update_kernel(counts_hbm, final_ref, states_hbm, out_hbm, counts_ref, states_ref, done_ref, counts_sem, states_sem, done_sem, root_ref, inverse_ref):
     link = lax.axis_index("link")
     own_rows, members = done_ref.shape
     half = members // 2
@@ -482,7 +505,7 @@
         [jnp.concatenate([head, upper], axis=1), jnp.concatenate([upper.T, tail], axis=1)], axis=0
     )
     forcing = jnp.concatenate([first, second], axis=1)
-    high, low = split(transform_of(gram, forcing))
+    high, low = split(transform_of(gram, forcing, root_ref, inverse_ref))
     fetch.wait()
     fetch_counts.wait()
     block_rows = states_hbm.shape[0] // counts_ref.shape[0]
@@ -495,8 +518,8 @@
 
     for index in range(blocks):
         states = states_ref[index * block_rows : (index + 1) * block_rows]
-        updated = jnp.dot(states, low, preferred_element_type=F32) + jnp.dot(
-            states, high, preferred_element_type=F32
+        updated = jnp.dot(
+            jnp.concatenate([states, states], axis=1), jnp.concatenate([low, high], axis=0), preferred_element_type=F32
         )
         living = position < counts_ref[link * blocks + index]
         done_ref[index * block_rows : (index + 1) * block_rows] = jnp.where(
@@ -590,6 +613,8 @@
             dma,
             dma,
             dma((own_rows // block_rows,)),
+            pltpu.VMEM((members, members), F32),
+            pltpu.VMEM((members, members), F32),
         ],
         compiler_params=grant,
     )(live_counts, pltpu.with_memory_space_constraint(gram, pltpu.VMEM), background)

time: 37.2 us -> 37 us (level)
  Pallas kernels: 37 us -> 36.6 us
    pallas_call x1, Pallas kernels: 3.98 us -> 3.56 us  [per_device(): pl.pallas_call(update_kernel, out_shape=jax.ShapeDtypeStruct((own_rows, m...]
where the time goes in v5:
time: 37 us; the launch traced here: 36.6 us
  Pallas kernels  36.6 us (99%)
    pallas_call x1, Pallas kernels, per_device(): pl.pallas_call(functools.partial(gram_kernel, n_orig, n_link, cuts), out_...  33.1 us
    pallas_call x1, Pallas kernels, per_device(): pl.pallas_call(update_kernel, out_shape=jax.ShapeDtypeStruct((own_rows, m...  3.56 us

profile of v5, /device:TPU:0, one launch (start us, length us, event | category | flops | bytes accessed | tf_op | source)
XLA Modules:
  0.0 36.6 jit_solution(8126053621386993863)
XLA Ops:
  0.0 33.1 %shard_map.73.final_ref = f32[2,16,9,128]{3,2,1,0:T(8,128)S(1)} custom-call(s32[12,1,16]{2,1,0:T(1,128)} %bitcast.4, s32[12,1,16]{2,1,0:T(1,128)} %bitcast.5, s32[16]{0:T(128)} %counts_hbm.3, bf16[32,128,128]{2,1,0:T(8,128)(2,1)} %bitcast.3, bf16[2048,256]{1,0:T(8,128)(2,1)} %states_hbm.3, f32[1,128]{1,0:T(1,128)} %obs_hbm.1, f32[1,128]{1,0:T(1,128)} %var_hbm.1), custom_call_target="tpu_custom_call" | custom-call | tf_op jit(solution)/shard_map/pallas_call | solution.py:555
  33.1 3.6 %shard_map.74 = bf16[512,256]{1,0:T(8,128)(2,1)} custom-call(s32[16]{0:T(128)} %counts_hbm.3, f32[2,16,9,128]{3,2,1,0:T(8,128)S(1)} %shard_map.73.final_ref, bf16[2048,256]{1,0:T(8,128)(2,1)} %states_hbm.3), custom_call_target="tpu_custom_call" | custom-call | tf_op jit(solution)/shard_map/pallas_call | solution.py:604

commit v6 on v5

--- a/solution.py
+++ b/solution.py
@@ -156,8 +156,9 @@
     column = lax.broadcasted_iota(jnp.int32, (members, members), 1)
     identity = (row == column).astype(F32)
     system = identity + gram * (1.0 / (members - 1.0))
-    bound = jnp.max(jnp.sum(jnp.abs(system), axis=1, keepdims=True), axis=0, keepdims=True)
-    root = system / bound
+    bound = jnp.max(jnp.sum(jnp.abs(system), axis=0, keepdims=True), axis=1, keepdims=True)
+    shrink = 1.0 / bound
+    root = system * shrink
     middle = 1.5 * identity - 0.5 * root
     inverse_ref[...] = middle
     root_ref[...] = mm3(root, middle)
@@ -173,10 +174,13 @@
     lax.fori_loop(1, NS_ITERS - 1, sweep, 0)
     inverse = inverse_ref[...]
     inverse = mm3(1.5 * identity - 0.5 * mm3(inverse, root_ref[...]), inverse)
+    scale = 1.0 / jnp.sqrt(bound)
+    share = shrink / (members - 1.0)
     inner = jnp.sum(inverse * column_of(forcing), axis=0, keepdims=True)
-    mean_weights = jnp.sum(inverse * inner, axis=1, keepdims=True) / (bound * (members - 1.0))
-    whole = inverse / jnp.sqrt(bound) + mean_weights
-    return whole + (1.0 - jnp.sum(whole, axis=0, keepdims=True)) / members
+    mean_weights = jnp.sum(inverse * inner, axis=1, keepdims=True) * share
+    across = jnp.sum(inverse, axis=0, keepdims=True)
+    total = across * scale + jnp.sum(across * inner, axis=1, keepdims=True) * share
+    return inverse * scale + (1.0 - total) / members + mean_weights
 
 
 def gram_kernel(
@@ -422,6 +426,16 @@
 
     repeat(ring - 1, scatter_start)
 
+    def first_end(step):
+        first(step, 1).wait_send()
+        first(step, 0).wait_send()
+        beside(step).wait_send()
+
+    rolled(steps, first_end)
+    rolled(remote, lambda step: beyond(step).wait_send())
+    swap.wait_send()
+
+
     def reduce_piece():
         def arrive(step):
             scatter(step).wait_recv()
@@ -444,6 +458,10 @@
 
     guarded(rank < owners, reduce_piece)
 
+    def scatter_end(step):
+        guarded(xor(rank, ring - 1 - step, ring) < owners, lambda: scatter(step).wait_send())
+
+    rolled(ring - 1, scatter_end)
     def spread_wait(step):
         other = xor(rank, ring - 1 - step, ring)
         guarded(other < owners, lambda: spread_out(other, step, other).wait_recv())
@@ -454,29 +472,17 @@
         send_sem=send6, recv_sem=recv6, device_id=(orig, twin), device_id_type=MESH,
     )
     share.start()
-    share.wait_recv()
-
-    out_ref[...] = final_ref[...]
-
-    def first_end(step):
-        first(step, 1).wait_send()
-        first(step, 0).wait_send()
-        beside(step).wait_send()
-
-    rolled(steps, first_end)
-    rolled(remote, lambda step: beyond(step).wait_send())
-    swap.wait_send()
-
-    def scatter_end(step):
-        guarded(xor(rank, ring - 1 - step, ring) < owners, lambda: scatter(step).wait_send())
-
-    rolled(ring - 1, scatter_end)
     guarded(
         rank < owners,
         lambda: rolled(
             ring - 1, lambda step: spread_out(rank, step, xor(rank, ring - 1 - step, ring)).wait_send()
         ),
     )
+    share.wait_recv()
+
+    out_ref[...] = final_ref[...]
+
+
     share.wait_send()
 
 

time: 37 us -> 36.7 us (level)
  no operation moved by 1% of the time
where the time goes in v6:
time: 36.7 us; the launch traced here: 36.6 us
  Pallas kernels  36.6 us (100%)
    pallas_call x1, Pallas kernels, per_device(): pl.pallas_call(functools.partial(gram_kernel, n_orig, n_link, cuts), out_...  33 us
    pallas_call x1, Pallas kernels, per_device(): pl.pallas_call(update_kernel, out_shape=jax.ShapeDtypeStruct((own_rows, m...  3.53 us

profile of v6, /device:TPU:0, one launch (start us, length us, event | category | flops | bytes accessed | tf_op | source)
XLA Modules:
  0.0 36.6 jit_solution(17147595521565478570)
XLA Ops:
  0.0 33.0 %shard_map.73.final_ref = f32[2,16,9,128]{3,2,1,0:T(8,128)S(1)} custom-call(s32[12,1,16]{2,1,0:T(1,128)} %bitcast.4, s32[12,1,16]{2,1,0:T(1,128)} %bitcast.5, s32[16]{0:T(128)} %counts_hbm.3, bf16[32,128,128]{2,1,0:T(8,128)(2,1)} %bitcast.3, bf16[2048,256]{1,0:T(8,128)(2,1)} %states_hbm.3, f32[1,128]{1,0:T(1,128)} %obs_hbm.1, f32[1,128]{1,0:T(1,128)} %var_hbm.1), custom_call_target="tpu_custom_call" | custom-call | tf_op jit(solution)/shard_map/pallas_call | solution.py:561
  33.0 3.5 %shard_map.74 = bf16[512,256]{1,0:T(8,128)(2,1)} custom-call(s32[16]{0:T(128)} %counts_hbm.3, f32[2,16,9,128]{3,2,1,0:T(8,128)S(1)} %shard_map.73.final_ref, bf16[2048,256]{1,0:T(8,128)(2,1)} %states_hbm.3), custom_call_target="tpu_custom_call" | custom-call | tf_op jit(solution)/shard_map/pallas_call | solution.py:610

commit v7 on v6

--- a/solution.py
+++ b/solution.py
@@ -367,7 +367,7 @@
         beyond(step).wait_recv()
         sums[pairs - 1, cut(step)] = sums[pairs - 1, cut(step)] + far_in[step // cuts, cut(step)]
 
-    repeat(remote, gather)
+    rolled(remote, gather)
 
     load_small[3].wait()
     load_small[4].wait()

time: 36.7 us -> 36.7 us (level)
  no operation moved by 1% of the time
where the time goes in v7:
time: 36.7 us; the launch traced here: 36.6 us
  Pallas kernels  36.5 us (99%)
    pallas_call x1, Pallas kernels, per_device(): pl.pallas_call(functools.partial(gram_kernel, n_orig, n_link, cuts), out_...  33 us
    pallas_call x1, Pallas kernels, per_device(): pl.pallas_call(update_kernel, out_shape=jax.ShapeDtypeStruct((own_rows, m...  3.53 us

profile of v7, /device:TPU:0, one launch (start us, length us, event | category | flops | bytes accessed | tf_op | source)
XLA Modules:
  0.0 36.6 jit_solution(14981497525558052995)
XLA Ops:
  0.0 33.0 %shard_map.73.final_ref = f32[2,16,9,128]{3,2,1,0:T(8,128)S(1)} custom-call(s32[12,1,16]{2,1,0:T(1,128)} %bitcast.4, s32[12,1,16]{2,1,0:T(1,128)} %bitcast.5, s32[16]{0:T(128)} %counts_hbm.3, bf16[32,128,128]{2,1,0:T(8,128)(2,1)} %bitcast.3, bf16[2048,256]{1,0:T(8,128)(2,1)} %states_hbm.3, f32[1,128]{1,0:T(1,128)} %obs_hbm.1, f32[1,128]{1,0:T(1,128)} %var_hbm.1), custom_call_target="tpu_custom_call" | custom-call | tf_op jit(solution)/shard_map/pallas_call | solution.py:561
  33.0 3.5 %shard_map.74 = bf16[512,256]{1,0:T(8,128)(2,1)} custom-call(s32[16]{0:T(128)} %counts_hbm.3, f32[2,16,9,128]{3,2,1,0:T(8,128)S(1)} %shard_map.73.final_ref, bf16[2048,256]{1,0:T(8,128)(2,1)} %states_hbm.3), custom_call_target="tpu_custom_call" | custom-call | tf_op jit(solution)/shard_map/pallas_call | solution.py:610
